TPU v7x, 512 devices: a whole 4x8x8 slice. The times are simulated.
512 devices in a mesh: enc: 16 (over y, x_lo), slab: 32 (over x_hi, z, core).
Axes of the slice: x: 4 (x_hi: 2, x_lo: 2; x = x_hi * 2 + x_lo), y: 8, z: 8, core: 2. Of those that a mesh axis runs over, the one named last changes fastest.
Arguments:
- tokens: bfloat16 [32768, 1024], P(('slab', 'enc')), may hold values from -6 to 6
- cotangent: bfloat16 [32768, 1024], P(('slab', 'enc')), may hold values from -6 to 6
- w_qkv: bfloat16 [1024, 3072], P('slab', 'enc'), may hold values from -0.5 to 0.5
- w_out: bfloat16 [1024, 1024], P('enc', 'slab'), may hold values from -0.1875 to 0.1875
- mod_scale: float32 [1024], replicated, may hold values from -0.5 to 0.5
- mod_shift: float32 [1024], replicated, may hold values from -0.5 to 0.5
- mod_gate: float32 [1024], replicated, may hold values from 0.5 to 1.5
- counts: int32 [64], P('slab'), may hold values from 64 to 512
- edge_index: int32 [64, 128], P('slab'), may hold values from 0 to 1023
Outputs:
- grad_tokens: bfloat16 [32768, 1024], P(('slab', 'enc'))
- grad_qkv: float32 [1024, 3072], P('slab', 'enc')
- grad_out: float32 [1024, 1024], P('enc', 'slab')
Inputs may be any that keep to these rules, and one draw needn't show every extreme that they name: The first counts[w] slots of window w hold voxels; the rest are padding. `edge_index`: A row index within the preceding slab's 2 * 512 rows.
All inputs are finite; a program needn't handle non-finite values.
Results may differ from a plain program's by a relative error of at most 0.023.
Values may be sent and summed in bfloat16 or wider, within the bound.
A program may use at most 64 MiB of HBM per device.

v0:
```python
import jax
import jax.numpy as jnp
from jax import lax
from jax.sharding import PartitionSpec as P

HD = 64
EPS = 1e-06


def in_one_piece(arrays, axis, dim, along):
    widths = [a.shape[along] for a in arrays]
    both = jnp.concatenate(arrays, axis=along)
    whole = lax.all_gather(both, axis, axis=dim, tiled=True)
    return tuple(jnp.split(whole, [sum(widths[:k]) for k in range(1, len(widths))], axis=along))


def turned_gather(arrays, axis, dims):
    turned = [jnp.moveaxis(a, dim, 0) for a, dim in zip(arrays, dims)]
    widths = [t[0].size for t in turned]
    both = jnp.concatenate([t.reshape(-1, w) for t, w in zip(turned, widths)], axis=1)
    whole = lax.all_gather(both, axis, axis=0, tiled=True)
    blocks = jnp.split(whole, [sum(widths[:k]) for k in range(1, len(widths))], axis=1)
    return tuple(
        (
            jnp.moveaxis(b.reshape(-1, *t.shape[1:]), 0, dim)
            for b, t, dim in zip(blocks, turned, dims)
        )
    )


def shifted(block, axis, distance):
    devices = range(lax.axis_size(axis))
    route = [(i - distance, i) for i in devices if i - distance in devices]
    return lax.ppermute(block, axis, route)


def in_blocks(array, dim, peers):
    before, after = (array.shape[:dim], array.shape[dim + 1 :])
    return jnp.moveaxis(array.reshape(*before, peers, -1, *after), dim, 0)


def sum_at_owner(array, axis, dim):
    blocks = in_blocks(array, dim, lax.axis_size(axis))
    arrived = lax.all_to_all(blocks, axis, split_axis=0, concat_axis=0, tiled=True)
    return arrived.astype(jnp.float32).sum(axis=0)


def statistics(features):
    widened = features.astype(jnp.float32)
    average = jnp.mean(widened, 1, keepdims=True)
    centred = widened - average
    variance = jnp.mean(centred * centred, 1, keepdims=True)
    inv_std = lax.rsqrt(variance + EPS)
    return (centred * inv_std, inv_std)


def attend(query, key_vals, edge_vals, counts, edge_live, upstream, out_rows):
    windows = counts.shape[0]
    row_count = query.shape[0]
    win_size = row_count // windows
    head_size = query.shape[1]
    factor = head_size ** (-0.5)
    query_win = query.reshape(windows, win_size, head_size)
    keys_all = jnp.concatenate([key_vals.reshape(windows, win_size, 2 * head_size), edge_vals], 1)
    key_part = keys_all[:, :, :head_size]
    value_part = keys_all[:, :, head_size:]
    position = jnp.arange(win_size, dtype=jnp.int32)
    own_live = position[None, :] < counts[:, None]
    key_live = jnp.concatenate(
        [own_live, jnp.broadcast_to(edge_live[:, None], (windows, edge_vals.shape[1]))], 1
    )
    row_live = own_live.astype(jnp.float32)[:, :, None]
    scores = (
        jnp.einsum("wqd,wkd->wqk", query_win, key_part, preferred_element_type=jnp.float32) * factor
    )
    scores = jnp.where(key_live[:, None, :], scores, -1000000000.0)
    largest = jnp.max(scores, -1, keepdims=True)
    exponent = jnp.exp(scores - largest)
    softmax_p = exponent / jnp.sum(exponent, -1, keepdims=True)
    weights_b = softmax_p.astype(jnp.bfloat16)
    attended = (
        jnp.einsum("wqk,wkd->wqd", weights_b, value_part, preferred_element_type=jnp.float32)
        * row_live
    )
    attended = attended.astype(jnp.bfloat16).reshape(row_count, head_size)
    grad_att = jnp.dot(upstream, out_rows.T, preferred_element_type=jnp.float32).reshape(
        windows, win_size, head_size
    )
    grad_att = (grad_att * row_live).astype(jnp.bfloat16)
    grad_prob = jnp.einsum("wqd,wkd->wqk", grad_att, value_part, preferred_element_type=jnp.float32)
    grad_value = jnp.einsum("wqk,wqd->wkd", weights_b, grad_att, preferred_element_type=jnp.float32)
    grad_score = (
        softmax_p * (grad_prob - jnp.sum(grad_prob * softmax_p, -1, keepdims=True)) * factor
    )
    grad_score = grad_score.astype(jnp.bfloat16)
    grad_query = jnp.einsum(
        "wqk,wkd->wqd", grad_score, key_part, preferred_element_type=jnp.float32
    )
    grad_key = jnp.einsum("wqk,wqd->wkd", grad_score, query_win, preferred_element_type=jnp.float32)
    grad_pair = jnp.concatenate([grad_key, grad_value], -1)
    own_pair = grad_pair[:, :win_size].reshape(row_count, 2 * head_size)
    return (attended, grad_query.reshape(row_count, head_size), own_pair, grad_pair[:, win_size:])


def on_device(tokens, cotangent, w_qkv, w_out, mod_scale, mod_shift, mod_gate, counts, edge_index):
    features, upstream_in = in_one_piece((tokens, cotangent), "enc", 0, 1)
    weight_in, weight_out = turned_gather((w_qkv, w_out), "slab", (0, 1))
    normal_x, inv_std = statistics(features)
    gain = 1.0 + mod_scale
    normed = (normal_x * gain + mod_shift).astype(jnp.bfloat16)
    upstream = (upstream_in.astype(jnp.float32) * mod_gate).astype(jnp.bfloat16)
    windows = counts.shape[0]
    edge_count = edge_index.shape[1]
    heads_here = weight_out.shape[0] // HD
    pair_width = 2 * HD
    projected = jnp.dot(normed, weight_in, preferred_element_type=jnp.float32).astype(jnp.bfloat16)
    key_vals = projected[:, HD : 3 * HD]
    slab_index = lax.axis_index("slab")
    edge_live = jnp.full((windows,), slab_index > 0)
    flat_index = edge_index.reshape(-1)
    next_index = shifted(flat_index, "slab", -1)
    picked = jnp.take(key_vals, next_index, axis=0)
    edge_vals = shifted(picked, "slab", 1)
    edge_vals = edge_vals.reshape(windows, edge_count, heads_here * pair_width)
    attended, grad_query, own_pair, edge_pair = attend(
        projected[:, :HD], projected[:, HD:], edge_vals, counts, edge_live, upstream, weight_out
    )
    own_grads = own_pair
    edge_grads = edge_pair.reshape(-1, heads_here * pair_width)
    returned = shifted(edge_grads.astype(jnp.bfloat16), "slab", -1).astype(edge_grads.dtype)
    own_grads = own_grads.at[next_index].add(returned)
    grad_proj = jnp.concatenate([grad_query, own_grads], 1).astype(jnp.bfloat16)
    grad_q_local = jnp.dot(normed.T, grad_proj, preferred_element_type=jnp.float32)
    grad_o_local = jnp.dot(attended.T, upstream, preferred_element_type=jnp.float32)
    partial_value = jnp.dot(grad_proj, weight_in.T, preferred_element_type=jnp.float32)
    own_rows = tokens.shape[0]
    row_start = lax.axis_index("enc") * own_rows
    normal_own = lax.dynamic_slice_in_dim(normal_x, row_start, own_rows, 0)
    inv_own = lax.dynamic_slice_in_dim(inv_std, row_start, own_rows, 0)
    mine = sum_at_owner(partial_value.astype(jnp.bfloat16), "enc", 0)
    grad_hat = mine * gain
    grad_tokens = cotangent.astype(jnp.float32) + inv_own * (
        grad_hat
        - jnp.mean(grad_hat, 1, keepdims=True)
        - normal_own * jnp.mean(grad_hat * normal_own, 1, keepdims=True)
    )
    grad_qkv, grad_out = (
        sum_at_owner(grad_q_local.astype(jnp.bfloat16), "slab", 0),
        sum_at_owner(grad_o_local.astype(jnp.bfloat16), "slab", 1),
    )
    return (grad_tokens.astype(jnp.bfloat16), grad_qkv, grad_out)


def solution(mesh):
    placed = (
        P(("slab", "enc"), None),
        P(("slab", "enc"), None),
        P("slab", "enc"),
        P("enc", "slab"),
        P(),
        P(),
        P(),
        P("slab"),
        P("slab", None),
    )
    return jax.shard_map(
        on_device,
        mesh=mesh,
        in_specs=placed,
        out_specs=(P(("slab", "enc"), None), P("slab", "enc"), P("enc", "slab")),
        check_vma=False,
    )
```

profile of v0, /device:TPU:64, one launch (start us, length us, event | category | flops | bytes accessed | tf_op | source)
XLA Modules:
  0.0 280.1 jit_solution(14782367953100508507)
XLA Ops:
  8.9 1.9 collective-permute-start
  12.3 44.6 %all_gather.7 = bf16[1024,256]{1,0:T(8,128)(2,1)S(1)} all-gather(bf16[32,256]{1,0:T(8,128)(2,1)S(1)} %pad_maximum_fusion.8), channel_id=1, replica_groups=mesh['enc'=16,'slab'=32] {'slab'}, dimensions={0}, use_global_device_ids=true | all-gather | bytes 540672 | tf_op jit(solution)/shard_map/all_gather | solution.py:21
  58.3 57.7 %all-gather.2.cloned.1.call-done = bf16[1024,2048]{1,0:T(8,128)(2,1)} async-done(((bf16[64,2048]{1,0:T(8,128)(2,1)}), bf16[1024,2048]{1,0:T(8,128)(2,1)}) %all-gather.2.cloned.1.call-update) | async-done | bytes 4194320 | tf_op jit(solution)/shard_map/all_gather | solution.py:13
  116.0 2.1 convert_reduce_fusion
  118.1 2.3 fusion.4
  122.9 1.9 collective-permute-start.1
  124.8 3.1 %fusion.16 = f32[1024,64]{0,1:T(8,128)} fusion(bf16[1024,2048]{1,0:T(8,128)(2,1)} %all-gather.2.cloned.1.call-done, f32[1024]{0:T(1024)S(1)} %copy-done.6, bf16[1024,256]{1,0:T(8,128)(2,1)S(1)} %all_gather.7), kind=kOutput, calls=%fused_computation.22 | convolution fusion | flops 137363456 | bytes 2625536 | tf_op jit(solution)/shard_map/dot_general | solution.py:86
  131.0 4.0 %fusion.89 = (f32[2,512]{1,0:T(2,128)}, f32[2,512,640]{2,1,0:T(8,128)}) fusion(pred[2,640]{1,0:T(4,128)(4,1)} %concatenate.20, bf16[8,2,8,512]{3,2,1,0:T(8,128)(2,1)} %bitcast.62, bf16[2,512,128]{1,2,0:T(8,128)(2,1)S(1)} %bitcast.58, bf16[2,128,128]{1,2,0:T(8,128)(2,1)S(1)} %copy.19), kind=kOutput, calls=%fused_computation.94 | convolution fusion | flops 86835840 | bytes 3085568 | tf_op jit(solution)/shard_map/sub | solution.py:78
  135.1 2.3 fusion.29
  137.4 3.1 %fusion.27 = bf16[2,8,8,512]{3,2,1,0:T(8,128)(2,1)} fusion(f32[2,512]{1,0:T(2,128)S(1)} %get-tuple-element.6, bf16[2,128,128]{1,2,0:T(8,128)(2,1)S(1)} %copy.19, bf16[2,512,128]{1,2,0:T(8,128)(2,1)} %bitcast.56, f32[2,512]{1,0:T(2,128)} %get-tuple-element.7, pred[2,640]{1,0:T(4,128)(4,1)} %concatenate.20, bf16[8,2,8,512]{3,2,1,0:T(8,128)(2,1)} %bitcast.64), kind=kOutput, calls=%fused_computation.35 | convolution fusion | flops 171837056 | bytes 928256 | tf_op jit(solution)/shard_map/wqk,wkd->wqd/dot_general | solution.py:82
  140.4 8.7 %fusion.23 = bf16[2,512,64]{1,2,0:T(8,128)(2,1)} fusion(f32[2,512,640]{2,1,0:T(8,128)S(1)} %fusion.54, bf16[2,512,128]{1,2,0:T(8,128)(2,1)} %bitcast.57, bf16[2,128,128]{1,2,0:T(8,128)(2,1)S(1)} %copy.19, f32[2,512,640]{2,1,0:T(8,128)} %get-tuple-element.8, f32[2,512]{1,0:T(2,128)} %get-tuple-element.7), kind=kOutput, calls=%fused_computation.33 | convolution fusion | flops 88868480 | bytes 10952704 | tf_op jit(solution)/shard_map/wqk,wkd->wqd/dot_general | solution.py:96
  149.1 8.9 %fusion.10 = f32[2,640,64]{1,2,0:T(8,128)} fusion(f32[2,512,640]{2,1,0:T(8,128)S(1)} %fusion.54, bf16[8,2,8,512]{3,2,1,0:T(8,128)(2,1)} %bitcast.65, f32[2,512,640]{2,1,0:T(8,128)} %get-tuple-element.8, f32[2,512]{1,0:T(2,128)} %get-tuple-element.7), kind=kOutput, calls=%fused_computation.18 | convolution fusion | flops 88475264 | bytes 5705728 | tf_op jit(solution)/shard_map/wqk,wqd->wkd/dot_general | solution.py:99
  159.9 3.8 %collective-permute-start.2 = (bf16[256,128]{1,0:T(8,128)(2,1)S(1)}, bf16[256,128]{1,0:T(8,128)(2,1)S(1)}, u32[]{:S(2)}, u32[]{:S(2)}) collective-permute-start(bf16[256,128]{1,0:T(8,128)(2,1)S(1)} %bitcast.67), channel_id=1, source_target_pairs={{1,0},{2,1},{3,2},{4,3},{5,4},{6,5},{7,6},{8,7},{9,8},{10,9},{11,1... | collective-permute-start | bytes 196616 | tf_op jit(solution)/shard_map/ppermute | solution.py:34
  163.7 2.2 fusion.22
  167.2 11.2 %all-to-all-start.2 = ((bf16[32,2,1024]{2,1,0:T(2,128)(2,1)}), bf16[32,2,1024]{2,1,0:T(2,128)(2,1)S(1)}, u32[]{:S(2)}, u32[]{:S(2)}) async-start(bf16[32,2,1024]{2,1,0:T(2,128)(2,1)} %reshape.141), calls=%async_computation.2 | async-start | bytes 262144 | tf_op jit(solution)/shard_map/all_to_all | solution.py:44
  178.6 2.3 scatter_custom_fusion
  181.0 2.9 %convolution_convert_fusion.1 = bf16[1024,192]{0,1:T(8,128)(2,1)S(1)} fusion(f32[1024]{0:T(1024)S(1)} %copy-done.9, f32[1024]{0:T(1024)S(1)} %broadcast_add_fusion, bf16[1024,128]{1,0:T(8,128)(2,1)S(1)} %convert.12, bf16[1024,64]{1,0:T(8,128)(2,1)S(1)} %bitcast.52, f32[1024]{0:T(1024)S(1)} %add_rsqrt_fusion, f32[1024]{0:T(1024)S(1)} %broadcast_multiply_fusion, ...), kind=kOutput, calls=%fused_computation.29 | convolution fusion | flops 409927680 | bytes 2899968 | tf_op jit(solution)/shard_map/dot_general | solution.py:133
  184.9 4.4 %all-to-all-done.2 = bf16[32,2,1024]{2,1,0:T(2,128)(2,1)S(1)} async-done(((bf16[32,2,1024]{2,1,0:T(2,128)(2,1)}), bf16[32,2,1024]{2,1,0:T(2,128)(2,1)S(1)}, u32[]{:S(2)}, u32[]{:S(2)}) %all-to-all-start.2) | async-done | bytes 131104 | tf_op jit(solution)/shard_map/all_to_all | solution.py:44
  189.2 5.5 %all-to-all-start.1 = ((bf16[32,32,192]{2,1,0:T(8,128)(2,1)}), bf16[32,32,192]{2,1,0:T(8,128)(2,1)S(1)}, u32[]{:S(2)}, u32[]{:S(2)}) async-start(bf16[32,32,192]{2,1,0:T(8,128)(2,1)} %bitcast.7), calls=%async_computation.1 | async-start | bytes 1048576 | tf_op jit(solution)/shard_map/all_to_all | solution.py:44
  194.7 2.2 convolution_convert_fusion
  196.8 17.1 %all-to-all-done.1 = bf16[32,32,192]{2,1,0:T(8,128)(2,1)S(1)} async-done(((bf16[32,32,192]{2,1,0:T(8,128)(2,1)}), bf16[32,32,192]{2,1,0:T(8,128)(2,1)S(1)}, u32[]{:S(2)}, u32[]{:S(2)}) %all-to-all-start.1) | async-done | bytes 393248 | tf_op jit(solution)/shard_map/all_to_all | solution.py:44
  213.9 6.6 %all-to-all-start = ((bf16[16,64,1024]{2,1,0:T(8,128)(2,1)}), bf16[16,64,1024]{2,1,0:T(8,128)(2,1)S(1)}, u32[]{:S(2)}, u32[]{:S(2)}) async-start(bf16[16,64,1024]{2,1,0:T(8,128)(2,1)} %bitcast.6), calls=%async_computation | async-start | bytes 4194304 | tf_op jit(solution)/shard_map/all_to_all | solution.py:44
  220.6 4.1 %fusion.2 = f32[1024,1024]{1,0:T(8,128)} fusion(f32[1024]{0:T(1024)S(1)} %add_rsqrt_fusion, f32[1024]{0:T(1024)S(1)} %broadcast_multiply_fusion, bf16[1024,2048]{1,0:T(8,128)(2,1)} %all-gather.2.cloned.1.call-done), kind=kLoop, calls=%fused_computation.6 | loop fusion | flops 3145728 | bytes 6299648 | tf_op jit(solution)/shard_map/mul | solution.py:54
  226.3 43.7 %all-to-all-done = bf16[16,64,1024]{2,1,0:T(8,128)(2,1)S(1)} async-done(((bf16[16,64,1024]{2,1,0:T(8,128)(2,1)}), bf16[16,64,1024]{2,1,0:T(8,128)(2,1)S(1)}, u32[]{:S(2)}, u32[]{:S(2)}) %all-to-all-start) | async-done | bytes 2097184 | tf_op jit(solution)/shard_map/all_to_all | solution.py:44
  (62 shorter events, 19.4 us)
Async XLA Ops:
  7.2 108.8 %all-gather.2.cloned.1.call-start = ((), (), s32[]{:S(2)}) async-start(), calls=%async_computation.3 | async-start | bytes 4456448 | tf_op jit(solution)/shard_map/all_gather | solution.py:13
  8.9 111.5 %copy-start.8 = (f32[1024]{0:T(1024)S(1)}, f32[1024]{0:T(1024)}, u32[]{:S(2)}) copy-start(f32[1024]{0:T(1024)} %param.14) | copy-start | bytes 12292
  8.9 49.3 %collective-permute-start = (s32[256]{0:T(256)}, s32[256]{0:T(256)S(1)}, u32[]{:S(2)}, u32[]{:S(2)}) collective-permute-start(s32[256]{0:T(256)} %bitcast.70), channel_id=1, source_target_pairs={{1,0},{2,1},{3,2},{4,3},{5,4},{6,5},{7,6},{8,7},{9,8},{10,9},{11,1... | collective-permute-start | bytes 3080 | tf_op jit(solution)/shard_map/ppermute | solution.py:34
  58.2 57.7 %copy-start.5 = (s32[256]{0:T(256)}, s32[256]{0:T(256)S(1)}, u32[]{:S(2)}) copy-start(s32[256]{0:T(256)S(1)} %compare_select_fusion) | copy-start | bytes 3076
  116.0 4.4 %copy-start = (bf16[1024,2048]{1,0:T(8,128)(2,1)S(1)}, bf16[1024,2048]{1,0:T(8,128)(2,1)}, u32[]{:S(2)}) copy-start(bf16[1024,2048]{1,0:T(8,128)(2,1)} %all-gather.2.cloned.1.call-done) | copy-start | bytes 12582916
  120.4 4.4 %copy-start.6 = (f32[1024]{0:T(1024)S(1)}, f32[1024]{0:T(1024)}, u32[]{:S(2)}) copy-start(f32[1024]{0:T(1024)} %param.15) | copy-start | bytes 12292
  122.9 6.5 %collective-permute-start.1 = (bf16[256,128]{1,0:T(8,128)(2,1)S(1)}, bf16[256,128]{1,0:T(8,128)(2,1)S(1)}, u32[]{:S(2)}, u32[]{:S(2)}) collective-permute-start(bf16[256,128]{1,0:T(8,128)(2,1)S(1)} %broadcast_select_fusion), channel_id=1, source_target_pairs={{0,1},{1,2},{2,3},{3,4},{4,5},{5,6},{6,7},{7,8},{8,9},{9,10},{10,1... | collective-permute-start | bytes 196616 | tf_op jit(solution)/shard_map/ppermute | solution.py:34
  129.3 1.7 copy-start.2
  149.1 14.7 %copy-start.7 = (f32[1024]{0:T(1024)S(1)}, f32[1024]{0:T(1024)}, u32[]{:S(2)}) copy-start(f32[1024]{0:T(1024)} %param.15) | copy-start | bytes 12292
  157.9 8.0 %copy-start.1 = (f32[2,640,64]{1,2,0:T(8,128)S(1)}, f32[2,640,64]{1,2,0:T(8,128)}, u32[]{:S(2)}) copy-start(f32[2,640,64]{1,2,0:T(8,128)} %fusion.10) | copy-start | bytes 983044
  159.9 18.7 %collective-permute-start.2 = (bf16[256,128]{1,0:T(8,128)(2,1)S(1)}, bf16[256,128]{1,0:T(8,128)(2,1)S(1)}, u32[]{:S(2)}, u32[]{:S(2)}) collective-permute-start(bf16[256,128]{1,0:T(8,128)(2,1)S(1)} %bitcast.67), channel_id=1, source_target_pairs={{1,0},{2,1},{3,2},{4,3},{5,4},{6,5},{7,6},{8,7},{9,8},{10,9},{11,1... | collective-permute-start | bytes 196616 | tf_op jit(solution)/shard_map/ppermute | solution.py:34
  163.7 14.7 %copy-start.4 = (bf16[2,512,64]{1,2,0:T(8,128)(2,1)S(1)}, bf16[2,512,64]{1,2,0:T(8,128)(2,1)}, u32[]{:S(2)}) copy-start(bf16[2,512,64]{1,2,0:T(8,128)(2,1)} %fusion.23) | copy-start | bytes 393220
  165.9 15.0 %copy-start.9 = (f32[1024]{0:T(1024)S(1)}, f32[1024]{0:T(1024)}, u32[]{:S(2)}) copy-start(f32[1024]{0:T(1024)} %param.14) | copy-start | bytes 12292
  167.2 22.0 %all-to-all-start.2 = ((bf16[32,2,1024]{2,1,0:T(2,128)(2,1)}), bf16[32,2,1024]{2,1,0:T(2,128)(2,1)S(1)}, u32[]{:S(2)}, u32[]{:S(2)}) async-start(bf16[32,2,1024]{2,1,0:T(2,128)(2,1)} %reshape.141), calls=%async_computation.2 | async-start | bytes 262144 | tf_op jit(solution)/shard_map/all_to_all | solution.py:44
  189.2 24.7 %all-to-all-start.1 = ((bf16[32,32,192]{2,1,0:T(8,128)(2,1)}), bf16[32,32,192]{2,1,0:T(8,128)(2,1)S(1)}, u32[]{:S(2)}, u32[]{:S(2)}) async-start(bf16[32,32,192]{2,1,0:T(8,128)(2,1)} %bitcast.7), calls=%async_computation.1 | async-start | bytes 1048576 | tf_op jit(solution)/shard_map/all_to_all | solution.py:44
  213.9 56.0 %all-to-all-start = ((bf16[16,64,1024]{2,1,0:T(8,128)(2,1)}), bf16[16,64,1024]{2,1,0:T(8,128)(2,1)S(1)}, u32[]{:S(2)}, u32[]{:S(2)}) async-start(bf16[16,64,1024]{2,1,0:T(8,128)(2,1)} %bitcast.6), calls=%async_computation | async-start | bytes 4194304 | tf_op jit(solution)/shard_map/all_to_all | solution.py:44
  224.7 46.8 %copy-start.3 = (bf16[64,1024]{1,0:T(8,128)(2,1)S(1)}, bf16[64,1024]{1,0:T(8,128)(2,1)}, u32[]{:S(2)}) copy-start(bf16[64,1024]{1,0:T(8,128)(2,1)} %param.10) | copy-start | bytes 393220
Sparse Core Ops, SparseCore 0:
  10.1 105.8 all-gather.1
where the time goes:
time: 281 us; the launch traced here: 280 us
  waiting for transfers between devices  123 us (44%)
  blocking collectives  44.6 us (16%)
  matrix products  40.1 us (14%)
  starting transfers between devices  30.9 us (11%)
  other arithmetic  20.3 us (7%)
  between operations  14.4 us (5%)
  local copies, waits for them, and re-layouts  6.96 us (2%)
    all_to_all x3, waiting for transfers between devices, sum_at_owner(): lax.all_to_all(blocks, axis, split_axis=0, concat_axis=0, tiled=True)  65.1 us
    all_gather x1, waiting for transfers between devices, in_one_piece(): whole = lax.all_gather(both, axis, axis=dim, tiled=True)  57.7 us
    all_gather x1, blocking collectives, turned_gather(): whole = lax.all_gather(both, axis, axis=0, tiled=True)  44.6 us
    all_to_all x3, starting transfers between devices, sum_at_owner(): lax.all_to_all(blocks, axis, split_axis=0, concat_axis=0, tiled=True)  23.2 us
    dot_general x1, matrix products, attend(): jnp.einsum('wqk,wqd->wkd', grad_score, query_win, preferred_element_type=...  8.88 us
    dot_general x1, matrix products, attend(): jnp.einsum('wqk,wkd->wqd', grad_score, key_part, preferred_element_type=j...  8.65 us
    ppermute x3, starting transfers between devices, shifted(): return lax.ppermute(block, axis, route)  7.67 us
  transfers between devices with their start and end apart: 7, of which 4 were waited for; matrix products, arithmetic and copies ran while one was open for 9% of the time, Pallas kernels for 0%

commit v1 on v0

--- a/solution.py
+++ b/solution.py
@@ -18,7 +18,9 @@
     turned = [jnp.moveaxis(a, dim, 0) for a, dim in zip(arrays, dims)]
     widths = [t[0].size for t in turned]
     both = jnp.concatenate([t.reshape(-1, w) for t, w in zip(turned, widths)], axis=1)
-    whole = lax.all_gather(both, axis, axis=0, tiled=True)
+    whole = jnp.concatenate(
+        lax.all_to_all(jnp.stack([both] * lax.axis_size(axis)), axis, 0, 0), axis=0
+    )
     blocks = jnp.split(whole, [sum(widths[:k]) for k in range(1, len(widths))], axis=1)
     return tuple(
         (

time: 281 us -> 286 us (1.018)
  blocking collectives: 44.6 us -> 0 us
  waiting for transfers between devices: 123 us -> 158 us
  starting transfers between devices: 30.9 us -> 43.4 us
    all_gather x1 -> x0, blocking collectives: 44.6 us -> none  [turned_gather(): whole = lax.all_gather(both, axis, axis=0, tiled=True)]
    all_gather x1, waiting for transfers between devices: 57.7 us -> 92.7 us  [in_one_piece(): whole = lax.all_gather(both, axis, axis=dim, tiled=True)]
    all_to_all x0 -> x1, starting transfers between devices: none -> 12.8 us  [turned_gather(): lax.all_to_all(jnp.stack([both] * lax.axis_size(axis)), axis, 0, 0)]
  transfers between devices with their start and end apart: 7 -> 8, of which waited for: 4 -> 4; matrix products, arithmetic and copies ran while one was open for 9% -> 11% of each run, Pallas kernels for 0% -> 0%
where the time goes in v1:
time: 286 us; the launch traced here: 285 us
  waiting for transfers between devices  158 us (55%)
  starting transfers between devices  43.4 us (15%)
  matrix products  41.6 us (15%)
  other arithmetic  20.2 us (7%)
  between operations  14.4 us (5%)
  local copies, waits for them, and re-layouts  7.81 us (3%)
    all_gather x1, waiting for transfers between devices, in_one_piece(): whole = lax.all_gather(both, axis, axis=dim, tiled=True)  92.7 us
    all_to_all x3, waiting for transfers between devices, sum_at_owner(): lax.all_to_all(blocks, axis, split_axis=0, concat_axis=0, tiled=True)  65.1 us
    all_to_all x3, starting transfers between devices, sum_at_owner(): lax.all_to_all(blocks, axis, split_axis=0, concat_axis=0, tiled=True)  22.9 us
    all_to_all x1, starting transfers between devices, turned_gather(): lax.all_to_all(jnp.stack([both] * lax.axis_size(axis)), axis, 0, 0)  12.8 us
    dot_general x1, matrix products, attend(): jnp.einsum('wqk,wqd->wkd', grad_score, query_win, preferred_element_type=...  8.88 us
    dot_general x1, matrix products, attend(): jnp.einsum('wqk,wkd->wqd', grad_score, key_part, preferred_element_type=j...  8.65 us
    ppermute x3, starting transfers between devices, shifted(): return lax.ppermute(block, axis, route)  7.67 us
  transfers between devices with their start and end apart: 8, of which 4 were waited for; matrix products, arithmetic and copies ran while one was open for 11% of the time, Pallas kernels for 0%

profile of v1, /device:TPU:64, one launch (start us, length us, event | category | flops | bytes accessed | tf_op | source)
XLA Modules:
  0.0 285.2 jit_solution(13491893945591762261)
XLA Ops:
  8.9 1.9 collective-permute-start
  12.5 12.8 %all-to-all-start = ((bf16[32,32,256]{2,1,0:T(8,128)(2,1)}), bf16[32,32,256]{2,1,0:T(8,128)(2,1)S(1)}, u32[]{:S(2)}, u32[]{:S(2)}) async-start(bf16[32,32,256]{2,1,0:T(8,128)(2,1)} %stack.2), calls=%async_computation | async-start | bytes 1048576 | tf_op jit(solution)/shard_map/all_to_all | solution.py:22
  27.4 92.7 %all-gather.2.cloned.1.call-done = bf16[1024,2048]{1,0:T(8,128)(2,1)} async-done(((bf16[64,2048]{1,0:T(8,128)(2,1)}), bf16[1024,2048]{1,0:T(8,128)(2,1)}) %all-gather.2.cloned.1.call-update) | async-done | bytes 4194320 | tf_op jit(solution)/shard_map/all_gather | solution.py:13
  120.1 1.9 convert_reduce_fusion
  122.0 2.3 fusion.4
  124.3 2.8 convolution_convert_fusion.2
  130.3 3.1 %fusion.16 = f32[1024,64]{0,1:T(8,128)} fusion(bf16[1024,2048]{1,0:T(8,128)(2,1)} %all-gather.2.cloned.1.call-done, f32[1024]{0:T(1024)S(1)} %copy-done.5, bf16[1024,256]{1,0:T(8,128)(2,1)S(1)} %bitcast.54), kind=kOutput, calls=%fused_computation.22 | convolution fusion | flops 137363456 | bytes 2625536 | tf_op jit(solution)/shard_map/dot_general | solution.py:88
  136.5 4.0 %fusion.89 = (f32[2,512]{1,0:T(2,128)}, f32[2,512,640]{2,1,0:T(8,128)}) fusion(pred[2,640]{1,0:T(4,128)(4,1)} %concatenate.20, bf16[8,2,8,512]{3,2,1,0:T(8,128)(2,1)} %bitcast.66, bf16[2,512,128]{1,2,0:T(8,128)(2,1)S(1)} %bitcast.62, bf16[2,128,128]{1,2,0:T(8,128)(2,1)S(1)} %copy.19), kind=kOutput, calls=%fused_computation.94 | convolution fusion | flops 86835840 | bytes 3085568 | tf_op jit(solution)/shard_map/sub | solution.py:80
  140.6 2.3 fusion.29
  142.9 3.1 %fusion.27 = bf16[2,8,8,512]{3,2,1,0:T(8,128)(2,1)} fusion(f32[2,512]{1,0:T(2,128)S(1)} %get-tuple-element.6, bf16[2,128,128]{1,2,0:T(8,128)(2,1)S(1)} %copy.19, bf16[2,512,128]{1,2,0:T(8,128)(2,1)} %bitcast.60, f32[2,512]{1,0:T(2,128)} %get-tuple-element.7, pred[2,640]{1,0:T(4,128)(4,1)} %concatenate.20, bf16[8,2,8,512]{3,2,1,0:T(8,128)(2,1)} %bitcast.68), kind=kOutput, calls=%fused_computation.35 | convolution fusion | flops 171837056 | bytes 928256 | tf_op jit(solution)/shard_map/wqk,wkd->wqd/dot_general | solution.py:84
  145.9 8.7 %fusion.23 = bf16[2,512,64]{1,2,0:T(8,128)(2,1)} fusion(f32[2,512,640]{2,1,0:T(8,128)S(1)} %fusion.54, bf16[2,512,128]{1,2,0:T(8,128)(2,1)} %bitcast.61, bf16[2,128,128]{1,2,0:T(8,128)(2,1)S(1)} %copy.19, f32[2,512,640]{2,1,0:T(8,128)} %get-tuple-element.8, f32[2,512]{1,0:T(2,128)} %get-tuple-element.7), kind=kOutput, calls=%fused_computation.33 | convolution fusion | flops 88868480 | bytes 10952704 | tf_op jit(solution)/shard_map/wqk,wkd->wqd/dot_general | solution.py:98
  154.6 8.9 %fusion.10 = f32[2,640,64]{1,2,0:T(8,128)} fusion(f32[2,512,640]{2,1,0:T(8,128)S(1)} %fusion.54, bf16[8,2,8,512]{3,2,1,0:T(8,128)(2,1)} %bitcast.69, f32[2,512,640]{2,1,0:T(8,128)} %get-tuple-element.8, f32[2,512]{1,0:T(2,128)} %get-tuple-element.7), kind=kOutput, calls=%fused_computation.18 | convolution fusion | flops 88475264 | bytes 5705728 | tf_op jit(solution)/shard_map/wqk,wqd->wkd/dot_general | solution.py:101
  165.4 3.8 %collective-permute-start.2 = (bf16[256,128]{1,0:T(8,128)(2,1)S(1)}, bf16[256,128]{1,0:T(8,128)(2,1)S(1)}, u32[]{:S(2)}, u32[]{:S(2)}) collective-permute-start(bf16[256,128]{1,0:T(8,128)(2,1)S(1)} %bitcast.71), channel_id=1, source_target_pairs={{1,0},{2,1},{3,2},{4,3},{5,4},{6,5},{7,6},{8,7},{9,8},{10,9},{11,1... | collective-permute-start | bytes 196616 | tf_op jit(solution)/shard_map/ppermute | solution.py:36
  169.2 2.2 fusion.22
  172.7 11.5 %all-to-all-start.3 = ((bf16[32,2,1024]{2,1,0:T(2,128)(2,1)}), bf16[32,2,1024]{2,1,0:T(2,128)(2,1)S(1)}, u32[]{:S(2)}, u32[]{:S(2)}) async-start(bf16[32,2,1024]{2,1,0:T(2,128)(2,1)} %reshape.147), calls=%async_computation.3 | async-start | bytes 262144 | tf_op jit(solution)/shard_map/all_to_all | solution.py:46
  184.4 2.3 scatter_custom_fusion
  186.7 2.9 %convolution_convert_fusion.1 = bf16[1024,192]{0,1:T(8,128)(2,1)S(1)} fusion(f32[1024]{0:T(1024)S(1)} %copy-done.8, f32[1024]{0:T(1024)S(1)} %broadcast_add_fusion, bf16[1024,128]{1,0:T(8,128)(2,1)S(1)} %convert.12, bf16[1024,64]{1,0:T(8,128)(2,1)S(1)} %bitcast.56, f32[1024]{0:T(1024)S(1)} %add_rsqrt_fusion, f32[1024]{0:T(1024)S(1)} %broadcast_multiply_fusion, ...), kind=kOutput, calls=%fused_computation.29 | convolution fusion | flops 409927680 | bytes 2899968 | tf_op jit(solution)/shard_map/dot_general | solution.py:135
  190.6 4.4 %all-to-all-done.3 = bf16[32,2,1024]{2,1,0:T(2,128)(2,1)S(1)} async-done(((bf16[32,2,1024]{2,1,0:T(2,128)(2,1)}), bf16[32,2,1024]{2,1,0:T(2,128)(2,1)S(1)}, u32[]{:S(2)}, u32[]{:S(2)}) %all-to-all-start.3) | async-done | bytes 131104 | tf_op jit(solution)/shard_map/all_to_all | solution.py:46
  195.0 5.5 %all-to-all-start.2 = ((bf16[32,32,192]{2,1,0:T(8,128)(2,1)}), bf16[32,32,192]{2,1,0:T(8,128)(2,1)S(1)}, u32[]{:S(2)}, u32[]{:S(2)}) async-start(bf16[32,32,192]{2,1,0:T(8,128)(2,1)} %bitcast.8), calls=%async_computation.2 | async-start | bytes 1048576 | tf_op jit(solution)/shard_map/all_to_all | solution.py:46
  200.5 2.2 convolution_convert_fusion
  202.6 17.1 %all-to-all-done.2 = bf16[32,32,192]{2,1,0:T(8,128)(2,1)S(1)} async-done(((bf16[32,32,192]{2,1,0:T(8,128)(2,1)}), bf16[32,32,192]{2,1,0:T(8,128)(2,1)S(1)}, u32[]{:S(2)}, u32[]{:S(2)}) %all-to-all-start.2) | async-done | bytes 393248 | tf_op jit(solution)/shard_map/all_to_all | solution.py:46
  219.7 6.0 %all-to-all-start.1 = ((bf16[16,64,1024]{2,1,0:T(8,128)(2,1)}), bf16[16,64,1024]{2,1,0:T(8,128)(2,1)S(1)}, u32[]{:S(2)}, u32[]{:S(2)}) async-start(bf16[16,64,1024]{2,1,0:T(8,128)(2,1)} %bitcast.7), calls=%async_computation.1 | async-start | bytes 4194304 | tf_op jit(solution)/shard_map/all_to_all | solution.py:46
  225.8 4.1 %fusion.2 = f32[1024,1024]{1,0:T(8,128)} fusion(f32[1024]{0:T(1024)S(1)} %add_rsqrt_fusion, f32[1024]{0:T(1024)S(1)} %broadcast_multiply_fusion, bf16[1024,2048]{1,0:T(8,128)(2,1)} %all-gather.2.cloned.1.call-done), kind=kLoop, calls=%fused_computation.6 | loop fusion | flops 3145728 | bytes 6299648 | tf_op jit(solution)/shard_map/mul | solution.py:56
  231.5 43.7 %all-to-all-done.1 = bf16[16,64,1024]{2,1,0:T(8,128)(2,1)S(1)} async-done(((bf16[16,64,1024]{2,1,0:T(8,128)(2,1)}), bf16[16,64,1024]{2,1,0:T(8,128)(2,1)S(1)}, u32[]{:S(2)}, u32[]{:S(2)}) %all-to-all-start.1) | async-done | bytes 2097184 | tf_op jit(solution)/shard_map/all_to_all | solution.py:46
  (62 shorter events, 20.9 us)
Async XLA Ops:
  7.2 112.9 %all-gather.2.cloned.1.call-start = ((), (), s32[]{:S(2)}) async-start(), calls=%async_computation.4 | async-start | bytes 4456448 | tf_op jit(solution)/shard_map/all_gather | solution.py:13
  8.9 18.4 %collective-permute-start = (s32[256]{0:T(256)}, s32[256]{0:T(256)S(1)}, u32[]{:S(2)}, u32[]{:S(2)}) collective-permute-start(s32[256]{0:T(256)} %bitcast.74), channel_id=1, source_target_pairs={{1,0},{2,1},{3,2},{4,3},{5,4},{6,5},{7,6},{8,7},{9,8},{10,9},{11,1... | collective-permute-start | bytes 3080 | tf_op jit(solution)/shard_map/ppermute | solution.py:36
  12.5 111.8 %copy-start.7 = (f32[1024]{0:T(1024)S(1)}, f32[1024]{0:T(1024)}, u32[]{:S(2)}) copy-start(f32[1024]{0:T(1024)} %param.14) | copy-start | bytes 12292
  12.5 111.8 %all-to-all-start = ((bf16[32,32,256]{2,1,0:T(8,128)(2,1)}), bf16[32,32,256]{2,1,0:T(8,128)(2,1)S(1)}, u32[]{:S(2)}, u32[]{:S(2)}) async-start(bf16[32,32,256]{2,1,0:T(8,128)(2,1)} %stack.2), calls=%async_computation | async-start | bytes 1048576 | tf_op jit(solution)/shard_map/all_to_all | solution.py:22
  27.4 92.7 %copy-start.4 = (s32[256]{0:T(256)}, s32[256]{0:T(256)S(1)}, u32[]{:S(2)}) copy-start(s32[256]{0:T(256)S(1)} %compare_select_fusion) | copy-start | bytes 3076
  124.3 6.0 %copy-start.5 = (f32[1024]{0:T(1024)S(1)}, f32[1024]{0:T(1024)}, u32[]{:S(2)}) copy-start(f32[1024]{0:T(1024)} %param.15) | copy-start | bytes 12292
  128.4 6.5 %collective-permute-start.1 = (bf16[256,128]{1,0:T(8,128)(2,1)S(1)}, bf16[256,128]{1,0:T(8,128)(2,1)S(1)}, u32[]{:S(2)}, u32[]{:S(2)}) collective-permute-start(bf16[256,128]{1,0:T(8,128)(2,1)S(1)} %broadcast_select_fusion), channel_id=1, source_target_pairs={{0,1},{1,2},{2,3},{3,4},{4,5},{5,6},{6,7},{7,8},{8,9},{9,10},{10,1... | collective-permute-start | bytes 196616 | tf_op jit(solution)/shard_map/ppermute | solution.py:36
  134.8 1.7 copy-start.1
  154.6 14.7 %copy-start.6 = (f32[1024]{0:T(1024)S(1)}, f32[1024]{0:T(1024)}, u32[]{:S(2)}) copy-start(f32[1024]{0:T(1024)} %param.15) | copy-start | bytes 12292
  163.4 8.0 %copy-start = (f32[2,640,64]{1,2,0:T(8,128)S(1)}, f32[2,640,64]{1,2,0:T(8,128)}, u32[]{:S(2)}) copy-start(f32[2,640,64]{1,2,0:T(8,128)} %fusion.10) | copy-start | bytes 983044
  165.4 19.0 %collective-permute-start.2 = (bf16[256,128]{1,0:T(8,128)(2,1)S(1)}, bf16[256,128]{1,0:T(8,128)(2,1)S(1)}, u32[]{:S(2)}, u32[]{:S(2)}) collective-permute-start(bf16[256,128]{1,0:T(8,128)(2,1)S(1)} %bitcast.71), channel_id=1, source_target_pairs={{1,0},{2,1},{3,2},{4,3},{5,4},{6,5},{7,6},{8,7},{9,8},{10,9},{11,1... | collective-permute-start | bytes 196616 | tf_op jit(solution)/shard_map/ppermute | solution.py:36
  169.2 15.0 %copy-start.3 = (bf16[2,512,64]{1,2,0:T(8,128)(2,1)S(1)}, bf16[2,512,64]{1,2,0:T(8,128)(2,1)}, u32[]{:S(2)}) copy-start(bf16[2,512,64]{1,2,0:T(8,128)(2,1)} %fusion.23) | copy-start | bytes 393220
  171.4 15.3 %copy-start.8 = (f32[1024]{0:T(1024)S(1)}, f32[1024]{0:T(1024)}, u32[]{:S(2)}) copy-start(f32[1024]{0:T(1024)} %param.14) | copy-start | bytes 12292
  172.7 22.3 %all-to-all-start.3 = ((bf16[32,2,1024]{2,1,0:T(2,128)(2,1)}), bf16[32,2,1024]{2,1,0:T(2,128)(2,1)S(1)}, u32[]{:S(2)}, u32[]{:S(2)}) async-start(bf16[32,2,1024]{2,1,0:T(2,128)(2,1)} %reshape.147), calls=%async_computation.3 | async-start | bytes 262144 | tf_op jit(solution)/shard_map/all_to_all | solution.py:46
  195.0 24.7 %all-to-all-start.2 = ((bf16[32,32,192]{2,1,0:T(8,128)(2,1)}), bf16[32,32,192]{2,1,0:T(8,128)(2,1)S(1)}, u32[]{:S(2)}, u32[]{:S(2)}) async-start(bf16[32,32,192]{2,1,0:T(8,128)(2,1)} %bitcast.8), calls=%async_computation.2 | async-start | bytes 1048576 | tf_op jit(solution)/shard_map/all_to_all | solution.py:46
  219.7 55.4 %all-to-all-start.1 = ((bf16[16,64,1024]{2,1,0:T(8,128)(2,1)}), bf16[16,64,1024]{2,1,0:T(8,128)(2,1)S(1)}, u32[]{:S(2)}, u32[]{:S(2)}) async-start(bf16[16,64,1024]{2,1,0:T(8,128)(2,1)} %bitcast.7), calls=%async_computation.1 | async-start | bytes 4194304 | tf_op jit(solution)/shard_map/all_to_all | solution.py:46
  229.8 46.8 %copy-start.2 = (bf16[64,1024]{1,0:T(8,128)(2,1)S(1)}, bf16[64,1024]{1,0:T(8,128)(2,1)}, u32[]{:S(2)}) copy-start(bf16[64,1024]{1,0:T(8,128)(2,1)} %param.10) | copy-start | bytes 393220
Sparse Core Ops, SparseCore 0:
  10.1 109.9 all-gather.1
